TPU v7x, 32 devices: a whole 2x2x4 slice. The times are simulated.
32 devices in a mesh: gx: 4 (over x, core), gy: 8 (over z, y).
Axes of the slice: x: 2, y: 2, z: 4, core: 2. Of those that a mesh axis runs over, the one named last changes fastest.
Arguments:
- state: float32 [256, 2, 128, 128], P(('gx', 'gy')), may hold values from -6 to 6
- hamiltonian: float32 [2, 128, 128], replicated, may hold values from -0.5 to 0.5
- couplings: float32 [16, 128, 128], replicated, may hold values from -0.125 to 0.125
- bath_coef: float32 [2, 16], replicated, may hold values from 0.2 to 1
- bath_rate: float32 [16], replicated, may hold values from 0.02 to 0.2
- occupation: int32 [256, 16], P(('gx', 'gy')), may hold values from 0 to 5
- send_list: int32 [32, 32, 1], P(('gx', 'gy')), may hold values from -1 to 7
- up_index: int32 [256, 16], P(('gx', 'gy')), may hold values from -1 to 39
- down_index: int32 [256, 16], P(('gx', 'gy')), may hold values from -1 to 39
- step: float32 [1], replicated, may hold values from 0.5 to 1.5
Outputs:
- derivative: float32 [256, 2, 128, 128], P(('gx', 'gy'))
- advanced: float32 [256, 2, 128, 128], P(('gx', 'gy'))
All inputs are finite; a program needn't handle non-finite values.
Results may differ from a plain program's by a relative error of at most 0.0003.
Values sent between devices are 32-bit elements; how exact they have to be, the bound alone decides.
A program may use at most 256 MiB of HBM per device.

v0:
```python
import jax
import jax.numpy as jnp
from jax import lax
from jax.sharding import PartitionSpec as P


def left_product(matrix, rows):
    return jnp.einsum("ij,mcjl->mcil", matrix, rows, precision=lax.Precision.HIGHEST)


def right_product(rows, matrix):
    return jnp.einsum("mcij,jl->mcil", rows, matrix, precision=lax.Precision.HIGHEST)


def derive(
    local, buffer, occupation, up_index, down_index, hamiltonian, couplings, bath_coef, bath_rate
):
    counts = occupation.astype(local.dtype)
    modes = couplings.shape[0]
    rows = local.shape[0]
    joined = jnp.concatenate([up_index, down_index], axis=1).T.reshape(-1)
    picked = jnp.take(buffer, jnp.clip(joined, 0, buffer.shape[0] - 1), axis=0)
    picked = picked * (joined >= 0).astype(buffer.dtype)[:, None, None, None]
    picked = picked.reshape((2 * modes, rows) + local.shape[1:])
    stacked = jnp.concatenate([couplings, couplings], axis=0)
    lefts = jnp.einsum("kij,kmcjl->kmcil", stacked, picked, precision=lax.Precision.HIGHEST)
    rights = jnp.einsum("kmcij,kjl->kmcil", picked, stacked, precision=lax.Precision.HIGHEST)
    comm = jnp.sum(lefts[:modes] - rights[:modes], axis=0)
    left_low, right_low = (lefts[modes:], rights[modes:])
    coef_real = bath_coef[0][:, None, None, None]
    coef_imag = bath_coef[1][:, None, None, None]
    part_x = coef_real * (left_low[:, :, 0] - right_low[:, :, 0]) - coef_imag * (
        left_low[:, :, 1] + right_low[:, :, 1]
    )
    part_y = coef_real * (left_low[:, :, 1] - right_low[:, :, 1]) + coef_imag * (
        left_low[:, :, 0] + right_low[:, :, 0]
    )
    weight = counts.T[:, :, None, None]
    sum_x = jnp.sum(weight * part_x, axis=0)
    sum_y = jnp.sum(weight * part_y, axis=0)
    total = jnp.stack([comm[:, 1] + sum_y, -comm[:, 0] - sum_x], axis=1)
    ham_real, ham_imag = (hamiltonian[0], hamiltonian[1])
    real_part, imag_part = (local[:, 0:1], local[:, 1:2])
    left_real = left_product(ham_real, real_part) - left_product(ham_imag, imag_part)
    left_imag = left_product(ham_real, imag_part) + left_product(ham_imag, real_part)
    right_real = right_product(real_part, ham_real) - right_product(imag_part, ham_imag)
    right_imag = right_product(real_part, ham_imag) + right_product(imag_part, ham_real)
    comm_real = left_real - right_real
    comm_imag = left_imag - right_imag
    total = total + jnp.concatenate([comm_imag, -comm_real], axis=1)
    damping = jnp.sum(counts * bath_rate[None, :], axis=1)
    return total - damping[:, None, None, None] * local


def body(
    state,
    hamiltonian,
    couplings,
    bath_coef,
    bath_rate,
    occupation,
    send_list,
    up_index,
    down_index,
    step,
):
    peers = send_list.shape[1]
    chosen = send_list[0]
    outgoing = jnp.take(state, jnp.clip(chosen, 0, state.shape[0] - 1), axis=0)
    outgoing = outgoing * (chosen >= 0).astype(state.dtype)[:, :, None, None, None]
    arrived = lax.all_to_all(outgoing, ("gx", "gy"), split_axis=0, concat_axis=0, tiled=True)
    buffer = jnp.concatenate([state, arrived.reshape((-1,) + state.shape[1:])], axis=0)
    derivative = derive(
        state,
        buffer,
        occupation,
        up_index,
        down_index,
        hamiltonian,
        couplings,
        bath_coef,
        bath_rate,
    )
    square_sum = lax.psum(jnp.sum(derivative * derivative), ("gx", "gy"))
    count = state.shape[0] * peers * 2 * state.shape[2] * state.shape[3]
    rms = jnp.sqrt(square_sum / count + 1e-06)
    advanced = state + step[0] / rms * derivative
    return (derivative, advanced)


def solution(mesh):
    placed = (
        P(("gx", "gy"), None, None, None),
        P(),
        P(),
        P(),
        P(),
        P(("gx", "gy"), None),
        P(("gx", "gy"), None, None),
        P(("gx", "gy"), None),
        P(("gx", "gy"), None),
        P(),
    )
    return jax.shard_map(
        body,
        mesh=mesh,
        in_specs=placed,
        out_specs=(P(("gx", "gy"), None, None, None), P(("gx", "gy"), None, None, None)),
        check_vma=False,
    )
```

profile of v0, /device:TPU:0, one launch (start us, length us, event | category | flops | bytes accessed | tf_op | source)
XLA Modules:
  0.0 357.2 jit_solution(14691093859716630962)
XLA Ops:
  0.6 0.7 fusion.49
  1.3 0.7 fusion.48
  1.9 0.7 compare_and_fusion.1
  2.6 4.0 %gather_fusion = f32[32,2,128,128]{3,2,1,0:T(8,128)} fusion(f32[8,2,128,128]{3,2,1,0:T(8,128)} %param.10, s32[1024]{0:T(1024)S(1)} %pad_clamp_fusion.1), kind=kCustom, calls=%fused_computation | custom fusion | bytes 8388736 | tf_op jit(solution)/shard_map/jit(_take)/gather | solution.py:69
  6.7 5.1 %fusion.16 = f32[32,1,2,128,128]{4,3,2,1,0:T(8,128)} fusion(f32[32,2,128,128]{3,2,1,0:T(8,128)} %gather_fusion, f32[32]{0:T(128)S(1)} %fusion.48, pred[32]{0:T(512)(128)(4,1)S(1)} %compare_and_fusion.1), kind=kLoop, calls=%fused_computation.29 | loop fusion | flops 2097152 | bytes 8388768 | tf_op jit(solution)/shard_map/mul | solution.py:70
  11.8 7.5 %all-to-all-start = ((f32[32,1,2,128,128]{4,3,2,1,0:T(8,128)}), f32[32,1,2,128,128]{4,3,2,1,0:T(8,128)}, u32[]{:S(2)}, u32[]{:S(2)}) async-start(f32[32,1,2,128,128]{4,3,2,1,0:T(8,128)} %fusion.16), calls=%async_computation | async-start | bytes 8388608 | tf_op jit(solution)/shard_map/all_to_all | solution.py:71
  19.3 0.3 copy.74
  21.0 0.6 fusion.31
  21.7 0.6 fusion.19
  22.3 0.6 fusion.29
  22.9 0.6 fusion.17
  23.5 0.6 fusion.30
  24.1 0.6 fusion.28
  24.7 1.4 fusion.23
  26.1 1.4 fusion.21
  27.5 87.5 %all-to-all-done = f32[32,1,2,128,128]{4,3,2,1,0:T(8,128)} async-done(((f32[32,1,2,128,128]{4,3,2,1,0:T(8,128)}), f32[32,1,2,128,128]{4,3,2,1,0:T(8,128)}, u32[]{:S(2)}, u32[]{:S(2)}) %all-to-all-start) | async-done | bytes 4194336 | tf_op jit(solution)/shard_map/all_to_all | solution.py:71
  115.0 5.2 %pad_maximum_fusion = f32[40,2,128,128]{3,2,1,0:T(8,128)} fusion(f32[32,2,128,128]{3,2,1,0:T(8,128)} %bitcast.6, f32[8,2,128,128]{3,2,1,0:T(8,128)S(1)} %copy-done.3), kind=kLoop, calls=%fused_computation.27 | loop fusion | flops 1310720 | bytes 10485760 | tf_op jit(solution)/shard_map/concatenate | solution.py:72
  120.2 17.4 %gather_fusion.1 = f32[256,2,128,128]{3,2,1,0:T(8,128)} fusion(f32[40,2,128,128]{3,2,1,0:T(8,128)} %pad_maximum_fusion, s32[1024]{0:T(1024)S(1)} %pad_clamp_fusion), kind=kCustom, calls=%fused_computation.1 | custom fusion | bytes 67109888 | tf_op jit(solution)/shard_map/jit(_take)/gather | solution.py:22
  137.6 37.4 %fusion = f32[32,8,2,128,128]{4,3,2,1,0:T(8,128)} fusion(f32[32,8,2,128,128]{4,3,2,1,0:T(8,128)} %bitcast.146, f32[32,8]{1,0:T(8,128)S(1)} %copy.63, pred[32,8]{1,0:T(8,128)(4,1)S(1)} %copy.61, f32[16,128,128]{2,1,0:T(8,128)} %param.12), kind=kOutput, calls=%fused_computation.3 | convolution fusion | flops 12902203392 | bytes 68158720 | tf_op jit(solution)/shard_map/kmcij,kjl->kmcil/dot_general | solution.py:27
  175.0 57.6 %fusion.9 = f32[32,8,2,128,128]{3,4,2,1,0:T(8,128)} fusion(f32[32,8,2,128,128]{4,3,2,1,0:T(8,128)S(1)} %bitcast.147, f32[32,8]{1,0:T(8,128)S(1)} %copy.63, pred[32,8]{1,0:T(8,128)(4,1)S(1)} %copy.61, f32[16,128,128]{2,1,0:T(8,128)} %param.12), kind=kOutput, calls=%fused_computation.13 | convolution fusion | flops 12902203392 | bytes 68158720 | tf_op jit(solution)/shard_map/kij,kmcjl->kmcil/dot_general | solution.py:26
  232.6 11.7 %slice.71 = f32[16,8,2,128,128]{4,3,2,1,0:T(8,128)} slice(f32[32,8,2,128,128]{4,3,2,1,0:T(8,128)} %fusion), slice={[0:16], [0:8], [0:2], [0:128], [0:128]} | slice | bytes 33554432 | tf_op jit(solution)/shard_map/slice | solution.py:28
  244.3 10.8 %fusion.55 = (f32[16,8,1,128,128]{4,3,2,1,0:T(8,128)}, f32[16,8,1,128,128]{4,3,2,1,0:T(8,128)}) fusion(f32[32,8,2,128,128]{4,3,2,1,0:T(8,128)} %fusion), kind=kLoop, calls=%fused_computation.95 | loop fusion | bytes 33554432 | tf_op jit(solution)/shard_map/slice | solution.py:35
  255.1 9.2 %copy.101 = f32[16,8,1,128,128]{3,4,1,0,2:T(8,128)} copy(f32[16,8,1,128,128]{4,3,2,1,0:T(8,128)} %get-tuple-element.14) | data formatting | bytes 16777216
  264.4 17.6 %copy.98 = f32[16,8,2,128,128]{3,4,2,1,0:T(8,128)} copy(f32[16,8,2,128,128]{4,3,2,1,0:T(8,128)} %slice.71) | data formatting | bytes 33554432
  282.0 9.2 %copy.102 = f32[16,8,1,128,128]{3,4,1,0,2:T(8,128)} copy(f32[16,8,1,128,128]{4,3,2,1,0:T(8,128)} %get-tuple-element.15) | data formatting | bytes 16777216
  291.2 11.7 %fusion.2 = f32[8,2,128,128]{2,3,1,0:T(8,128)S(1)} fusion(f32[16,8,2,128,128]{3,4,2,1,0:T(8,128)} %copy.98, f32[32,8,2,128,128]{3,4,2,1,0:T(8,128)} %fusion.9), kind=kLoop, calls=%fused_computation.6 | loop fusion | flops 8126464 | bytes 34603008 | tf_op jit(solution)/shard_map/reduce_sum | solution.py:28
  302.9 1.3 copy-done.4
  304.3 11.2 %fusion.15 = (f32[8,128,128]{1,2,0:T(8,128)S(1)}, f32[8,128,128]{1,2,0:T(8,128)S(1)}) fusion(f32[16,8,1,128,128]{3,4,1,0,2:T(8,128)S(1)} %copy-done.4, f32[16,8,1,128,128]{3,4,1,0,2:T(8,128)} %copy.101, f32[32,8,2,128,128]{3,4,2,1,0:T(8,128)} %fusion.9, f32[16]{0:T(128)S(1)} %get-tuple-element.19, f32[16]{0:T(128)S(1)} %get-tuple-element.18, ...), kind=kLoop, calls=%fused_computation.24 | loop fusion | flops 29097984 | bytes 34603648 | tf_op jit(solution)/shard_map/reduce_sum | solution.py:40
  315.6 1.1 multiply_reduce_fusion
  316.7 37.0 %psum.7 = f32[]{:T(128)} all-reduce(f32[]{:T(128)} %get-tuple-element.10), channel_id=1, replica_groups=mesh['gx'=4,'gy'=8] {'gx','gy'}, use_global_device_ids=true, to_apply=%region_5.6 | all-reduce | flops 1 | bytes 8 | tf_op jit(solution)/shard_map/psum | solution.py:84
  354.4 1.3 copy.86
  355.8 1.3 copy.87
  (40 shorter events, 1.0 us)
Async XLA Ops:
  6.6 12.6 %copy-start.3 = (f32[8,2,128,128]{3,2,1,0:T(8,128)S(1)}, f32[8,2,128,128]{3,2,1,0:T(8,128)}, u32[]{:S(2)}) copy-start(f32[8,2,128,128]{3,2,1,0:T(8,128)} %param.10) | copy-start | bytes 3145732
  6.6 13.6 %copy-start.10 = (s32[8,16]{1,0:T(8,128)S(1)}, s32[8,16]{1,0:T(8,128)}, u32[]{:S(2)}) copy-start(s32[8,16]{1,0:T(8,128)} %param.15) | copy-start | bytes 1540
  6.6 13.7 %copy-start.8 = (s32[8,16]{1,0:T(8,128)S(1)}, s32[8,16]{1,0:T(8,128)}, u32[]{:S(2)}) copy-start(s32[8,16]{1,0:T(8,128)} %param.18) | copy-start | bytes 1540
  6.6 13.7 %copy-start.9 = (s32[8,16]{1,0:T(8,128)S(1)}, s32[8,16]{1,0:T(8,128)}, u32[]{:S(2)}) copy-start(s32[8,16]{1,0:T(8,128)} %param.17) | copy-start | bytes 1540
  6.6 14.3 %copy-start.12 = (f32[16]{0:T(128)S(1)}, f32[16]{0:T(128)}, u32[]{:S(2)}) copy-start(f32[16]{0:T(128)} %param.14) | copy-start | bytes 196
  6.7 14.4 %copy-start.5 = (f32[2,128,128]{2,1,0:T(8,128)S(1)}, f32[2,128,128]{2,1,0:T(8,128)}, u32[]{:S(2)}) copy-start(f32[2,128,128]{2,1,0:T(8,128)} %param.11) | copy-start | bytes 393220
  11.8 11.7 %copy-start.11 = (f32[2,16]{1,0:T(2,128)S(1)}, f32[2,16]{1,0:T(2,128)}, u32[]{:S(2)}) copy-start(f32[2,16]{1,0:T(2,128)} %param.13) | copy-start | bytes 388
  11.8 103.2 %all-to-all-start = ((f32[32,1,2,128,128]{4,3,2,1,0:T(8,128)}), f32[32,1,2,128,128]{4,3,2,1,0:T(8,128)}, u32[]{:S(2)}, u32[]{:S(2)}) async-start(f32[32,1,2,128,128]{4,3,2,1,0:T(8,128)} %fusion.16), calls=%async_computation | async-start | bytes 8388608 | tf_op jit(solution)/shard_map/all_to_all | solution.py:71
  19.6 100.6 %copy-start.1 = (f32[8,2,128,128]{2,3,0,1:T(8,128)}, f32[8,2,128,128]{2,3,0,1:T(8,128)S(1)}, u32[]{:S(2)}) copy-start(f32[8,2,128,128]{2,3,0,1:T(8,128)S(1)} %copy.74) | copy-start | bytes 3145732
  137.6 37.4 %copy-start = (f32[256,2,128,128]{3,2,1,0:T(8,128)S(1)}, f32[256,2,128,128]{3,2,1,0:T(8,128)}, u32[]{:S(2)}) copy-start(f32[256,2,128,128]{3,2,1,0:T(8,128)} %gather_fusion.1) | copy-start | bytes 100663296
  291.2 13.0 %copy-start.4 = (f32[16,8,1,128,128]{3,4,1,0,2:T(8,128)S(1)}, f32[16,8,1,128,128]{3,4,1,0,2:T(8,128)}, u32[]{:S(2)}) copy-start(f32[16,8,1,128,128]{3,4,1,0,2:T(8,128)} %copy.102) | copy-start | bytes 25165828
  304.2 11.3 %copy-start.2 = (f32[8,2,128,128]{2,3,0,1:T(8,128)S(1)}, f32[8,2,128,128]{2,3,0,1:T(8,128)}, u32[]{:S(2)}) copy-start(f32[8,2,128,128]{2,3,0,1:T(8,128)} %copy-done.1) | copy-start | bytes 3145732
  304.2 11.3 %copy-start.6 = (f32[8,1,128,128]{2,3,0,1:T(8,128)S(1)}, f32[8,1,128,128]{2,3,0,1:T(8,128)}, u32[]{:S(2)}) copy-start(f32[8,1,128,128]{2,3,0,1:T(8,128)} %fusion.23) | copy-start | bytes 1572868
  304.2 11.4 %copy-start.7 = (f32[8,1,128,128]{2,3,0,1:T(8,128)S(1)}, f32[8,1,128,128]{2,3,0,1:T(8,128)}, u32[]{:S(2)}) copy-start(f32[8,1,128,128]{2,3,0,1:T(8,128)} %fusion.21) | copy-start | bytes 1572868
where the time goes:
time: 359 us; the launch traced here: 357 us
  matrix products  101 us (28%)
  waiting for transfers between devices  87.5 us (24%)
  local copies, waits for them, and re-layouts  84.8 us (24%)
  blocking collectives  37 us (10%)
  other arithmetic  36.8 us (10%)
  starting transfers between devices  7.45 us (2%)
    all_to_all x1, waiting for transfers between devices, body(): lax.all_to_all(outgoing, ('gx', 'gy'), split_axis=0, concat_axis=0, tiled...  87.5 us
    dot_general x1, matrix products, derive(): jnp.einsum('kij,kmcjl->kmcil', stacked, picked, precision=lax.Precision.H...  57.6 us
    unnamed x32, local copies, waits for them, and re-layouts  40.4 us
    dot_general x1, matrix products, derive(): jnp.einsum('kmcij,kjl->kmcil', picked, stacked, precision=lax.Precision.H...  37.4 us
    psum x1, blocking collectives, body(): square_sum = lax.psum(jnp.sum(derivative * derivative), ('gx', 'gy'))  37 us
    gather x1, local copies, waits for them, and re-layouts, derive(): picked = jnp.take(buffer, jnp.clip(joined, 0, buffer.shape[0] - 1), axis=0)  17.4 us
    slice x1, local copies, waits for them, and re-layouts, derive(): comm = jnp.sum(lefts[:modes] - rights[:modes], axis=0)  11.7 us
    reduce_sum x1, other arithmetic, derive(): comm = jnp.sum(lefts[:modes] - rights[:modes], axis=0)  11.7 us
  transfers between devices with their start and end apart: 1, of which 1 were waited for; matrix products, arithmetic and copies ran while one was open for 2% of the time, Pallas kernels for 0%

commit v1 on v0

v1 whole, which is shorter than its diff:
```python
import functools

import jax
import jax.numpy as jnp
from jax import lax
from jax.experimental import pallas as pl
from jax.experimental.pallas import tpu as pltpu
from jax.sharding import PartitionSpec as P

AXES = ("gx", "gy")
MESH = pl.DeviceIdType.MESH


def split(value):
    high = value.astype(jnp.bfloat16)
    low = (value - high.astype(jnp.float32)).astype(jnp.bfloat16)
    return high, low


def put(n_size, mode, rows, xr, xi, yr, yi, x_hi, x_lo, y_all):
    start, size = rows
    at = pl.ds(mode * n_size + start, size)
    cols = pl.ds(mode * n_size, n_size)
    for part, value in enumerate((xr, xi)):
        high, low = split(value)
        lanes = pl.ds(part * n_size, n_size)
        x_hi[at, lanes] = high
        x_lo[at, lanes] = low
    for part, value in enumerate((yr, yi)):
        high, low = split(value)
        y_all[pl.ds(part * n_size + start, size), cols] = high
        y_all[pl.ds((2 + part) * n_size + start, size), cols] = low


def build_modes(n, offset, source, up, down, occ, coef, x_hi, x_lo, y_all):
    modes = up.shape[1]
    entries, n_size = source.shape[0], source.shape[2]
    chunk = 32
    for k in range(modes):
        iu = up[n, k] - offset
        iw = down[n, k] - offset
        has_u = jnp.logical_and(iu >= 0, iu < entries)
        has_w = jnp.logical_and(iw >= 0, iw < entries)
        mu = jnp.where(has_u, 1.0, 0.0).astype(jnp.float32)
        mw = jnp.where(has_w, occ[n, k], 0).astype(jnp.float32)
        iu = jnp.clip(iu, 0, entries - 1)
        iw = jnp.clip(iw, 0, entries - 1)
        a = mw * coef[0, k]
        b = mw * coef[1, k]
        for start in range(0, n_size, chunk):
            rows = pl.ds(start, chunk)
            ur, ui = source[iu, 0, rows, :], source[iu, 1, rows, :]
            wr, wi = source[iw, 0, rows, :], source[iw, 1, rows, :]
            p = ur * mu + a * wr
            q = b * wi
            r = ui * mu + a * wi
            s = b * wr
            put(n_size, k, (start, chunk), p - q, r + s, p + q, r - s, x_hi, x_lo, y_all)


def products(n_size, x_hi, x_lo, y_all, q_left, q_right):
    dot = functools.partial(jnp.dot, preferred_element_type=jnp.float32)
    both = dot(q_left[...], x_hi[...])
    left = both[:n_size] + both[n_size:] + dot(q_left[:n_size, :], x_lo[...])
    right = dot(y_all[...], q_right[...])
    two = 2 * n_size
    right = right[:two, :n_size] + right[:two, n_size:] + right[two:, :n_size]
    return left[:, :n_size] - right[:n_size], left[:, n_size:] - right[n_size:]


def local_kernel(up, down, occ, coef, rate, state, q_left, q_right, out, x_hi, x_lo, y_all):
    rows, modes = up.shape
    n_size = state.shape[2]

    @pl.loop(0, rows)
    def _(n):
        build_modes(n, 0, state, up, down, occ, coef, x_hi, x_lo, y_all)
        for start in range(0, n_size, 32):
            at = pl.ds(start, 32)
            re, im = state[n, 0, at, :], state[n, 1, at, :]
            put(n_size, modes, (start, 32), re, im, re, im, x_hi, x_lo, y_all)
            put(n_size, modes + 1, (start, 32), -im, re, -im, re, x_hi, x_lo, y_all)
        re, im = products(n_size, x_hi, x_lo, y_all, q_left, q_right)
        damping = jnp.float32(0)
        for k in range(modes):
            damping += occ[n, k].astype(jnp.float32) * rate[k]
        out[n, 0] = im - damping * state[n, 0]
        out[n, 1] = -re - damping * state[n, 1]


def remote_kernel(up, down, occ, coef, arrived, partial, q_left, q_right, out, squares, x_hi, x_lo, y_all):
    rows = up.shape[0]
    n_size = arrived.shape[2]
    squares[...] = jnp.zeros_like(squares)

    @pl.loop(0, rows)
    def _(n):
        build_modes(n, rows, arrived, up, down, occ, coef, x_hi, x_lo, y_all)
        re, im = products(n_size, x_hi, x_lo, y_all, q_left, q_right)
        re, im = partial[n, 0] + im, partial[n, 1] - re
        out[n, 0] = re
        out[n, 1] = im
        total = re * re + im * im
        squares[...] += jnp.sum(total.reshape(n_size // 8, 8, n_size), axis=0)


def pick_kernel(chosen, state, out, held, sem, load_sem):
    peers = chosen.shape[0]
    rows = state.shape[0]
    load = pltpu.make_async_copy(state, held.at[pl.ds(0, rows)], load_sem)
    load.start()
    held[rows] = jnp.zeros_like(held[rows])
    load.wait()
    copies = []
    for p in range(peers):
        at = chosen[p]
        at = jnp.where(at < 0, rows, jnp.minimum(at, rows - 1))
        copy = pltpu.make_async_copy(held.at[at], out.at[p], sem.at[p])
        copy.start()
        copies.append(copy)
    for copy in copies:
        copy.wait()


def sum_kernel(gx, gy, squares, out, gathered, send_sem, recv_sem):
    x, y = lax.axis_index("gx"), lax.axis_index("gy")
    me = x * gy + y
    count = gx * gy
    barrier = pltpu.get_barrier_semaphore()

    @pl.loop(1, count)
    def _(step):
        other = lax.rem(me + step, count)
        pl.semaphore_signal(barrier, inc=1, device_id=(other // gy, lax.rem(other, gy)), device_id_type=MESH)

    pl.semaphore_wait(barrier, count - 1)

    def copy_to(step):
        other = lax.rem(me + step, count)
        return pltpu.make_async_remote_copy(
            src_ref=squares,
            dst_ref=gathered.at[step],
            send_sem=send_sem.at[step],
            recv_sem=recv_sem.at[step],
            device_id=(other // gy, lax.rem(other, gy)),
            device_id_type=MESH,
        )

    @pl.loop(1, count)
    def _(step):
        copy_to(step).start()

    gathered[0] = squares[...]

    @pl.loop(1, count)
    def _(step):
        copy_to(step).wait()

    out[...] = jnp.sum(jnp.sum(gathered[...], axis=0), axis=(0, 1), keepdims=True) + jnp.zeros(out.shape, out.dtype)


def smem():
    return pl.BlockSpec(memory_space=pltpu.SMEM)


def vmem():
    return pl.BlockSpec(memory_space=pltpu.VMEM)


def operand_scratch(modes, n_size):
    depth = modes * n_size
    return [
        pltpu.VMEM((depth, 2 * n_size), jnp.bfloat16),
        pltpu.VMEM((depth, 2 * n_size), jnp.bfloat16),
        pltpu.VMEM((4 * n_size, depth), jnp.bfloat16),
    ]


def matrices_of(stack):
    n_size = stack.shape[1]
    high = lax.reduce_precision(stack, 8, 7)
    low = (stack - high).astype(jnp.bfloat16)
    high = high.astype(jnp.bfloat16)
    left = jnp.stack([high, low]).transpose(0, 2, 1, 3).reshape(2 * n_size, -1)
    right = jnp.stack([high, low], axis=2).reshape(-1, 2 * n_size)
    return left, right


def make_body(gx, gy):
    count = gx * gy

    def body(state, hamiltonian, couplings, bath_coef, bath_rate, occupation, send_list, up_index, down_index, step):
        rows, _, n_size, _ = state.shape
        modes = couplings.shape[0]
        chosen = send_list.reshape(-1)
        slots = chosen.shape[0]
        outgoing = pl.pallas_call(
            pick_kernel,
            out_shape=jax.ShapeDtypeStruct((slots,) + state.shape[1:], state.dtype),
            in_specs=[smem(), pl.BlockSpec(memory_space=pl.ANY)],
            out_specs=pl.BlockSpec(memory_space=pl.ANY),
            scratch_shapes=[
                pltpu.VMEM((rows + 1,) + state.shape[1:], state.dtype),
                pltpu.SemaphoreType.DMA((slots,)),
                pltpu.SemaphoreType.DMA,
            ],
            name="pick",
        )(chosen, state)
        arrived = lax.all_to_all(outgoing, AXES, split_axis=0, concat_axis=0, tiled=True)
        left, right = matrices_of(jnp.concatenate([couplings, hamiltonian], axis=0))
        pair = 2 * rows * n_size * n_size * n_size * 2
        partial = pl.pallas_call(
            local_kernel,
            out_shape=jax.ShapeDtypeStruct(state.shape, state.dtype),
            in_specs=[smem()] * 5 + [vmem()] * 3,
            out_specs=vmem(),
            scratch_shapes=operand_scratch(modes + 2, n_size),
            cost_estimate=pl.CostEstimate(flops=pair * (modes + 2) * 8, bytes_accessed=1 << 25, transcendentals=0),
            name="local",
        )(up_index, down_index, occupation, bath_coef, bath_rate, state, left, right)
        depth = modes * n_size
        derivative, squares = pl.pallas_call(
            remote_kernel,
            out_shape=(
                jax.ShapeDtypeStruct(state.shape, state.dtype),
                jax.ShapeDtypeStruct((8, n_size), state.dtype),
            ),
            in_specs=[smem()] * 4 + [vmem()] * 4,
            out_specs=(vmem(), vmem()),
            scratch_shapes=operand_scratch(modes, n_size),
            name="remote",
        )(up_index, down_index, occupation, bath_coef, arrived, partial, left[:, :depth], right[:depth])
        total = pl.pallas_call(
            functools.partial(sum_kernel, gx, gy),
            out_shape=jax.ShapeDtypeStruct((8, n_size), state.dtype),
            in_specs=[vmem()],
            out_specs=vmem(),
            scratch_shapes=[
                pltpu.VMEM((count, 8, n_size), state.dtype),
                pltpu.SemaphoreType.DMA((count,)),
                pltpu.SemaphoreType.DMA((count,)),
            ],
            compiler_params=pltpu.CompilerParams(collective_id=0, has_side_effects=True),
            name="total",
        )(squares)
        size = rows * count * 2 * n_size * n_size
        rms = jnp.sqrt(total[0, 0] / size + 1e-06)
        advanced = state + step[0] / rms * derivative
        return derivative, advanced

    return body


def solution(mesh):
    placed = (
        P(AXES, None, None, None),
        P(),
        P(),
        P(),
        P(),
        P(AXES, None),
        P(AXES, None, None),
        P(AXES, None),
        P(AXES, None),
        P(),
    )
    return jax.shard_map(
        make_body(mesh.shape["gx"], mesh.shape["gy"]),
        mesh=mesh,
        in_specs=placed,
        out_specs=(P(AXES, None, None, None), P(AXES, None, None, None)),
        check_vma=False,
    )
```

time: 359 us -> 143 us (0.40)
  matrix products: 101 us -> 0 us
  local copies, waits for them, and re-layouts: 84.8 us -> 7.93 us
  Pallas kernels: 0 us -> 52.6 us
  blocking collectives: 37 us -> 0 us
  other arithmetic: 36.8 us -> 3.24 us
  waiting for transfers between devices: 87.5 us -> 69.5 us
    dot_general x10 -> x0, matrix products: 101 us -> none  [the longest x1 57.6 us: derive(): jnp.einsum('kij,kmcjl->kmcil', stacked, picked, precision=lax.Precision.H...]
    pallas_call x0 -> x4, Pallas kernels: none -> 52.6 us  [the longest x1 20.1 us: body(): pl.pallas_call(remote_kernel, out_shape=(jax.ShapeDtypeStruct(state.shape...]
    unnamed x32 -> x11, local copies, waits for them, and re-layouts: 40.4 us -> 2.51 us
    psum x1 -> x0, blocking collectives: 37 us -> none  [body(): square_sum = lax.psum(jnp.sum(derivative * derivative), ('gx', 'gy'))]
    reduce_sum x4 -> x0, other arithmetic: 24 us -> none  [the longest x1 11.7 us: derive(): comm = jnp.sum(lefts[:modes] - rights[:modes], axis=0)]
    gather x2 -> x0, local copies, waits for them, and re-layouts: 21.4 us -> none  [the longest x1 17.4 us: derive(): picked = jnp.take(buffer, jnp.clip(joined, 0, buffer.shape[0] - 1), axis=0)]
    slice x2 -> x3, local copies, waits for them, and re-layouts: 22.5 us -> 3.39 us  [the longest x1 1.2 us: body(): rms = jnp.sqrt(total[0, 0] / size + 1e-06)]
    all_to_all x1, waiting for transfers between devices: 87.5 us -> 69.5 us  [body(): lax.all_to_all(outgoing, AXES, split_axis=0, concat_axis=0, tiled=True)]
  transfers between devices with their start and end apart: 1 -> 1, of which waited for: 1 -> 1; matrix products, arithmetic and copies ran while one was open for 2% -> 5% of each run, Pallas kernels for 0% -> 13%
where the time goes in v1:
time: 143 us
  waiting for transfers between devices  69.5 us (49%)
  Pallas kernels  52.6 us (37%)
  local copies, waits for them, and re-layouts  7.93 us (6%)
  starting transfers between devices  7.46 us (5%)
  other arithmetic  3.24 us (2%)
  between operations  2.12 us (1%)
    all_to_all x1, waiting for transfers between devices, body(): lax.all_to_all(outgoing, AXES, split_axis=0, concat_axis=0, tiled=True)  69.5 us
    pallas_call x1, Pallas kernels, body(): pl.pallas_call(remote_kernel, out_shape=(jax.ShapeDtypeStruct(state.shape...  20.1 us
    pallas_call x1, Pallas kernels, body(): pl.pallas_call(local_kernel, out_shape=jax.ShapeDtypeStruct(state.shape,...  17.9 us
    pallas_call x1, Pallas kernels, body(): pl.pallas_call(functools.partial(sum_kernel, gx, gy), out_shape=jax.Shape...  10.4 us
    all_to_all x1, starting transfers between devices, body(): lax.all_to_all(outgoing, AXES, split_axis=0, concat_axis=0, tiled=True)  7.46 us
    pallas_call x1, Pallas kernels, body(): pl.pallas_call(pick_kernel, out_shape=jax.ShapeDtypeStruct((slots,) + sta...  4.16 us
  transfers between devices with their start and end apart: 1, of which 1 were waited for; matrix products, arithmetic and copies ran while one was open for 5% of the time, Pallas kernels for 13%

profile of v1, /device:TPU:0, one launch (start us, length us, event | category | flops | bytes accessed | tf_op | source)
XLA Modules:
  0.0 142.8 jit_solution(16203036550014651702)
XLA Ops:
  0.6 4.2 %pick.1 = f32[32,2,128,128]{3,2,1,0:T(8,128)} custom-call(s32[32]{0:T(128)} %bitcast.36, f32[8,2,128,128]{3,2,1,0:T(8,128)} %state.3), custom_call_target="tpu_custom_call" | custom-call | tf_op jit(solution)/shard_map/pick/pallas_call | solution.py:197
  4.8 0.0 copy-start.1
  4.8 0.0 copy-start.3
  4.8 7.5 %all-to-all-start = ((f32[32,2,128,128]{3,2,1,0:T(8,128)}), f32[32,2,128,128]{3,2,1,0:T(8,128)}, u32[]{:S(2)}, u32[]{:S(2)}) async-start(f32[32,2,128,128]{3,2,1,0:T(8,128)} %pick.1), calls=%async_computation | async-start | bytes 8388608 | tf_op jit(solution)/shard_map/all_to_all | solution.py:209
  12.3 0.0 copy-done.1
  12.3 0.0 copy-done.3
  12.3 0.3 reduce-precision_convert_fusion.1
  12.6 0.1 maximum_bitcast_fusion
  12.7 0.8 copy.20
  13.6 0.2 copy.29
  13.7 0.0 copy-start
  13.7 0.3 reduce-precision_convert_fusion
  14.0 0.1 pad_maximum_fusion
  14.2 1.2 copy.16
  15.4 1.2 copy.28
  16.6 0.0 copy-done
  16.6 1.1 slice.16.q_left
  17.7 0.1 fusion.2
  17.8 1.1 copy.19
  18.9 1.1 copy.30
  20.7 17.9 %local.1.partial = f32[8,2,128,128]{3,2,1,0:T(8,128)} custom-call(s32[8,16]{1,0:T(8,128)} %up.3, s32[8,16]{1,0:T(8,128)} %down.3, s32[8,16]{1,0:T(8,128)} %occ.3, f32[2,16]{1,0:T(2,128)} %coef.3, f32[16]{0:T(128)} %rate.1, f32[8,2,128,128]{3,2,1,0:T(8,128)} %state.3, bf16[256,2304]{1,0:T(8,128)(2,1)} %bitcast.28, bf16[2304,256]{1,0:T(8,128)(2,1)} %bitcast.33), custom_call_target="tpu_custom_call" | custom-call | flops 9663676416 | bytes 33554432 | tf_op jit(solution)/shard_map/local/pallas_call | solution.py:212
  38.5 69.5 %all-to-all-done.arrived = f32[32,2,128,128]{3,2,1,0:T(8,128)} async-done(((f32[32,2,128,128]{3,2,1,0:T(8,128)}), f32[32,2,128,128]{3,2,1,0:T(8,128)}, u32[]{:S(2)}, u32[]{:S(2)}) %all-to-all-start) | async-done | bytes 4194336 | tf_op jit(solution)/shard_map/all_to_all | solution.py:209
  108.0 0.0 copy-start.2
  108.0 20.1 %remote.1 = (f32[8,2,128,128]{3,2,1,0:T(8,128)}, f32[8,128]{1,0:T(8,128)}) custom-call(s32[8,16]{1,0:T(8,128)} %up.3, s32[8,16]{1,0:T(8,128)} %down.3, s32[8,16]{1,0:T(8,128)} %occ.3, f32[2,16]{1,0:T(2,128)} %coef.3, f32[32,2,128,128]{3,2,1,0:T(8,128)} %all-to-all-done.arrived, f32[8,2,128,128]{3,2,1,0:T(8,128)} %local.1.partial, ...), custom_call_target="tpu_custom_call" | custom-call | tf_op jit(solution)/shard_map/remote/pallas_call | solution.py:222
  128.2 10.4 %total.1 = f32[8,128]{1,0:T(8,128)} custom-call(f32[8,128]{1,0:T(8,128)} %get-tuple-element.5.squares), custom_call_target="tpu_custom_call" | custom-call | tf_op jit(solution)/shard_map/total/pallas_call | solution.py:233
  138.6 1.2 slice.15
  140.5 0.0 copy-done.2
  140.5 2.3 %multiply_add_fusion = f32[8,2,128,128]{3,2,1,0:T(8,128)} fusion(f32[8,2,128,128]{3,2,1,0:T(8,128)S(1)} %copy-done.2, f32[8,2,128,128]{3,2,1,0:T(8,128)} %get-tuple-element.2, f32[]{:T(128)S(6)} %div.7), kind=kLoop, calls=%fused_computation.16 | loop fusion | flops 524288 | bytes 3145732 | tf_op jit(solution)/shard_map/add | solution.py:248
Async XLA Ops:
  4.8 7.5 %copy-start.1 = (f32[16,128,128]{2,1,0:T(8,128)S(1)}, f32[16,128,128]{2,1,0:T(8,128)}, u32[]{:S(2)}) copy-start(f32[16,128,128]{2,1,0:T(8,128)} %param.12) | copy-start | bytes 3145732
  4.8 7.5 %copy-start.3 = (f32[2,128,128]{2,1,0:T(8,128)S(1)}, f32[2,128,128]{2,1,0:T(8,128)}, u32[]{:S(2)}) copy-start(f32[2,128,128]{2,1,0:T(8,128)} %param.11) | copy-start | bytes 393220
  4.8 103.2 %all-to-all-start = ((f32[32,2,128,128]{3,2,1,0:T(8,128)}), f32[32,2,128,128]{3,2,1,0:T(8,128)}, u32[]{:S(2)}, u32[]{:S(2)}) async-start(f32[32,2,128,128]{3,2,1,0:T(8,128)} %pick.1), calls=%async_computation | async-start | bytes 8388608 | tf_op jit(solution)/shard_map/all_to_all | solution.py:209
  13.7 2.9 %copy-start = (bf16[32,8,18,128]{3,1,2,0:T(8,128)(2,1)}, bf16[32,8,18,128]{3,1,2,0:T(8,128)(2,1)S(1)}, u32[]{:S(2)}) copy-start(bf16[32,8,18,128]{3,1,2,0:T(8,128)(2,1)S(1)} %copy.29) | copy-start | bytes 3538948
  108.0 32.4 %copy-start.2 = (f32[8,2,128,128]{3,2,1,0:T(8,128)S(1)}, f32[8,2,128,128]{3,2,1,0:T(8,128)}, u32[]{:S(2)}) copy-start(f32[8,2,128,128]{3,2,1,0:T(8,128)} %state.3) | copy-start | bytes 3145732

commit v2 on v1

v2 whole, which is shorter than its diff:
```python
import functools

import jax
import jax.numpy as jnp
from jax import lax
from jax.experimental import pallas as pl
from jax.experimental.pallas import tpu as pltpu
from jax.sharding import PartitionSpec as P

AXES = ("gx", "gy")
MESH = pl.DeviceIdType.MESH


def split(value):
    high = value.astype(jnp.bfloat16)
    low = (value - high.astype(jnp.float32)).astype(jnp.bfloat16)
    return high, low


def put(n_size, mode, rows, xr, xi, yr, yi, x_hi, x_lo, y_all):
    start, size = rows
    at = pl.ds(mode * n_size + start, size)
    cols = pl.ds(mode * n_size, n_size)
    for part, value in enumerate((xr, xi)):
        high, low = split(value)
        lanes = pl.ds(part * n_size, n_size)
        x_hi[at, lanes] = high
        x_lo[at, lanes] = low
    for part, value in enumerate((yr, yi)):
        high, low = split(value)
        y_all[pl.ds(part * n_size + start, size), cols] = high
        y_all[pl.ds((2 + part) * n_size + start, size), cols] = low


def build_modes(n, offset, source, up, down, occ, coef, x_hi, x_lo, y_all):
    modes = up.shape[1]
    entries, _, size, n_size = source[0].shape
    chunk = min(32, size)
    for k in range(modes):
        iu = up[n, k] - offset
        iw = down[n, k] - offset
        has_u = jnp.logical_and(iu >= 0, iu < entries)
        has_w = jnp.logical_and(iw >= 0, iw < entries)
        mu = jnp.where(has_u, 1.0, 0.0).astype(jnp.float32)
        mw = jnp.where(has_w, occ[n, k], 0).astype(jnp.float32)
        iu = jnp.clip(iu, 0, entries - 1)
        iw = jnp.clip(iw, 0, entries - 1)
        a = mw * coef[0, k]
        b = mw * coef[1, k]
        for start in range(0, n_size, chunk):
            part, rows = source[start // size], pl.ds(start % size, chunk)
            ur, ui = part[iu, 0, rows, :], part[iu, 1, rows, :]
            wr, wi = part[iw, 0, rows, :], part[iw, 1, rows, :]
            p = ur * mu + a * wr
            q = b * wi
            r = ui * mu + a * wi
            s = b * wr
            put(n_size, k, (start, chunk), p - q, r + s, p + q, r - s, x_hi, x_lo, y_all)


def products(n_size, x_hi, x_lo, y_all, q_left, q_right):
    dot = functools.partial(jnp.dot, preferred_element_type=jnp.float32)
    both = dot(q_left[...], x_hi[...])
    left = both[:n_size] + both[n_size:] + dot(q_left[:n_size, :], x_lo[...])
    right = dot(y_all[...], q_right[...])
    two = 2 * n_size
    right = right[:two, :n_size] + right[:two, n_size:] + right[two:, :n_size]
    return left[:, :n_size] - right[:n_size], left[:, n_size:] - right[n_size:]


def fill_matrices(mode, matrix, q_left, q_right):
    n_size = matrix.shape[0]
    high, low = split(matrix)
    at = pl.ds(mode * n_size, n_size)
    q_left[pl.ds(0, n_size), at] = high
    q_left[pl.ds(n_size, n_size), at] = low
    q_right[at, pl.ds(0, n_size)] = high
    q_right[at, pl.ds(n_size, n_size)] = low


def kernel(
    gx, gy, length, halves,
    up, down, occ, coef, rate, step, lists, state, couplings, hamiltonian,
    derivative, advanced,
    below, above, stage, arrived, list_v, list_s, x_hi, x_lo, y_all, q_left, q_right, squares, gathered,
    load_sem, up_sem, down_sem, below_sem, above_sem, list_send, list_recv, list_load, plane_send, plane_recv, sum_send, sum_recv,
):
    rows, modes = up.shape
    n_size = state.shape[2]
    count = gx * gy
    side = gy // length
    columns = gx * side
    slots = arrived.shape[0] // count
    x, y = lax.axis_index("gx"), lax.axis_index("gy")
    me = x * gy + y
    z, yy = y // side, lax.rem(y, side)
    column = x * side + yy
    size = n_size // halves

    def place(at, level):
        return at // side, level * side + lax.rem(at, side)

    def strip(half):
        return pl.ds(half * size, size)

    barrier = pltpu.get_barrier_semaphore()

    def load(half):
        return pltpu.make_async_copy(state.at[:, :, strip(half)], below[0][half], load_sem.at[half])

    for half in range(halves):
        load(half).start()

    @pl.loop(1, count)
    def _(hop):
        other = lax.rem(me + hop, count)
        pl.semaphore_signal(barrier, inc=1, device_id=(other // gy, lax.rem(other, gy)), device_id_type=MESH)

    pl.semaphore_wait(barrier, count - 1)

    def relay(hop, half, way):
        held = below if way > 0 else above
        return pltpu.make_async_remote_copy(
            src_ref=(held if hop else below)[hop][half],
            dst_ref=held[hop + 1][half],
            send_sem=(up_sem if way > 0 else down_sem).at[hop, half],
            recv_sem=(below_sem if way > 0 else above_sem).at[hop + 1, half],
            device_id=place(column, z + way),
            device_id_type=MESH,
        )

    def hand(level, hop, half, slot):
        source = place(column, level)
        return pltpu.make_async_remote_copy(
            src_ref=stage.at[level, hop, slot, :, strip(half)],
            dst_ref=arrived.at[(source[0] * gy + source[1]) * slots + slot, :, strip(half)],
            send_sem=plane_send.at[level, hop, slot, half],
            recv_sem=plane_recv.at[level, hop, slot, half],
            device_id=place(lax.rem(column + hop, columns), z),
            device_id_type=MESH,
        )

    def send_lists(hop):
        return pltpu.make_async_remote_copy(
            src_ref=lists,
            dst_ref=list_v.at[z],
            send_sem=list_send.at[hop],
            recv_sem=list_recv.at[hop],
            device_id=place(column, lax.rem(z + hop, length)),
            device_id_type=MESH,
        )

    for hop in range(1, length):
        send_lists(hop).start()
    for half in range(halves):
        load(half).wait()

        @pl.when(z + 1 < length)
        def _():
            relay(0, half, 1).start()

        @pl.when(z > 0)
        def _():
            relay(0, half, -1).start()

    own = pltpu.make_async_copy(lists, list_s.at[z], list_load.at[0])
    own.start()
    own.wait()

    def chosen(held, level, at, slot):
        target = place(at, z)
        entry = (target[0] * gy + target[1]) * slots + slot
        pick = list_s[level, entry // 128, lax.rem(entry, 128)]
        keep = jnp.where(pick < 0, 0.0, 1.0).astype(jnp.float32)
        pick = jnp.clip(pick, 0, rows - 1)
        return held[pick] * keep

    def distribute(held, level, half):
        source = place(column, level)
        first = (source[0] * gy + source[1]) * slots
        for slot in range(slots):

            @pl.loop(1, columns)
            def _(hop):
                stage[level, hop, slot, :, strip(half), :] = chosen(held, level, lax.rem(column + hop, columns), slot)
                hand(level, hop, half, slot).start()

            arrived[first + slot, :, strip(half), :] = chosen(held, level, column, slot)

    for half in range(halves):
        distribute(below[0][half], z, half)

    def arrive(hop, half):
        low, high = z - hop, z + hop

        @pl.when(low >= 0)
        def _():
            relay(hop - 1, half, 1).wait_recv()
            if hop + 1 < length:

                @pl.when(z + 1 < length)
                def _():
                    relay(hop, half, 1).start()

        @pl.when(high < length)
        def _():
            relay(hop - 1, half, -1).wait_recv()
            if hop + 1 < length:

                @pl.when(z > 0)
                def _():
                    relay(hop, half, -1).start()

        @pl.when(low >= 0)
        def _():
            distribute(below[hop][half], low, half)

        @pl.when(high < length)
        def _():
            distribute(above[hop][half], high, half)

    for k in range(modes):
        fill_matrices(k, couplings[k], q_left, q_right)
    for k in range(2):
        fill_matrices(modes + k, hamiltonian[k], q_left, q_right)
    here = below[0]

    def local_part(n):
        build_modes(n, 0, here, up, down, occ, coef, x_hi, x_lo, y_all)
        chunk = min(32, size)
        for start in range(0, n_size, chunk):
            part, at = here[start // size], pl.ds(start % size, chunk)
            re, im = part[n, 0, at, :], part[n, 1, at, :]
            put(n_size, modes, (start, chunk), re, im, re, im, x_hi, x_lo, y_all)
            put(n_size, modes + 1, (start, chunk), -im, re, -im, re, x_hi, x_lo, y_all)
        re, im = products(n_size, x_hi, x_lo, y_all, q_left, q_right)
        damping = jnp.float32(0)
        for k in range(modes):
            damping += occ[n, k].astype(jnp.float32) * rate[k]
        for half in range(halves):
            at = slice(half * size, (half + 1) * size)
            derivative[n, 0, strip(half)] = im[at] - damping * here[half][n, 0]
            derivative[n, 1, strip(half)] = -re[at] - damping * here[half][n, 1]

    for hop in range(1, length):
        send_lists(hop).wait()
    for hop in range(1, length):
        level = lax.rem(z + hop, length)
        copy = pltpu.make_async_copy(list_v.at[level], list_s.at[level], list_load.at[hop])
        copy.start()
        copy.wait()

    share = rows // halves

    for half in range(halves):

        @pl.loop(0, share)
        def _(n):
            local_part(half * share + n)

        arrive(1, half)

    for hop in range(2, length):
        for half in range(halves):
            arrive(hop, half)

    for level in range(length):

        @pl.loop(1, columns)
        def _(hop):
            for slot in range(slots):
                for half in range(halves):
                    hand(level, hop, half, slot).wait_recv()

    squares[...] = jnp.zeros_like(squares)
    depth = modes * n_size

    @pl.loop(0, rows)
    def _(n):
        build_modes(n, rows, [arrived], up, down, occ, coef, x_hi, x_lo, y_all)
        ops = (x_hi.at[:depth], x_lo.at[:depth], y_all.at[:, :depth], q_left.at[:, :depth], q_right.at[:depth])
        re, im = products(n_size, *ops)
        re, im = derivative[n, 0] + im, derivative[n, 1] - re
        derivative[n, 0] = re
        derivative[n, 1] = im
        total = re * re + im * im
        squares[...] += jnp.sum(total.reshape(n_size // 8, 8, n_size), axis=0)

    def copy_to(hop):
        other = lax.rem(me + hop, count)
        return pltpu.make_async_remote_copy(
            src_ref=squares,
            dst_ref=gathered.at[hop],
            send_sem=sum_send.at[hop],
            recv_sem=sum_recv.at[hop],
            device_id=(other // gy, lax.rem(other, gy)),
            device_id_type=MESH,
        )

    @pl.loop(1, count)
    def _(hop):
        copy_to(hop).start()

    gathered[0] = squares[...]
    for level in range(length):

        @pl.loop(1, columns)
        def _(hop):
            for slot in range(slots):
                for half in range(halves):
                    hand(level, hop, half, slot).wait_send()

    for hop in range(length - 1):
        for half in range(halves):

            @pl.when(jnp.logical_and(z >= hop, z + 1 < length))
            def _():
                relay(hop, half, 1).wait_send()

            @pl.when(jnp.logical_and(z + hop < length, z > 0))
            def _():
                relay(hop, half, -1).wait_send()

    @pl.loop(1, count)
    def _(hop):
        copy_to(hop).wait()

    total = jnp.sum(jnp.sum(gathered[...], axis=0), axis=(0, 1), keepdims=True)
    scale = step[0] / jnp.sqrt(total / (rows * count * 2 * n_size * n_size) + 1e-06)

    @pl.loop(0, rows)
    def _(n):
        for part in range(2):
            for half in range(halves):
                value = here[half][n, part] + scale * derivative[n, part, strip(half)]
                advanced[n, part, strip(half)] = value


def smem():
    return pl.BlockSpec(memory_space=pltpu.SMEM)


def vmem():
    return pl.BlockSpec(memory_space=pltpu.VMEM)


def line_length(gx, gy):
    side = max(gx // 2, 1)
    return gy // side if gy % side == 0 else gy


def make_body(gx, gy):
    count = gx * gy
    length = line_length(gx, gy)
    columns = count // length

    def body(state, hamiltonian, couplings, bath_coef, bath_rate, occupation, send_list, up_index, down_index, step):
        rows, parts, n_size, _ = state.shape
        modes = couplings.shape[0]
        slots = send_list.shape[2]
        halves = 2 if rows % 2 == 0 and n_size % 16 == 0 else 1
        chosen = send_list.reshape(-1)
        lanes = 128
        deep = -(-chosen.shape[0] // (8 * lanes)) * 8
        lists = jnp.pad(chosen, (0, deep * lanes - chosen.shape[0])).reshape(deep, lanes)
        depth = (modes + 2) * n_size
        tile = state.shape[1:]
        piece = pltpu.VMEM((rows, parts, n_size // halves, n_size), state.dtype)
        strips = tuple((piece,) * halves for _ in range(length))
        f32, bf16, i32 = jnp.float32, jnp.bfloat16, jnp.int32
        dma = pltpu.SemaphoreType.DMA
        return pl.pallas_call(
            functools.partial(kernel, gx, gy, length, halves),
            out_shape=(jax.ShapeDtypeStruct(state.shape, f32), jax.ShapeDtypeStruct(state.shape, f32)),
            in_specs=[smem()] * 6 + [vmem(), pl.BlockSpec(memory_space=pl.ANY), vmem(), vmem()],
            out_specs=(vmem(), vmem()),
            scratch_shapes=[
                strips,
                ((pltpu.VMEM((1, 1, 8, n_size), f32),) * halves,) + strips[1:],
                pltpu.VMEM((length, columns, slots) + tile, f32),
                pltpu.VMEM((count * slots,) + tile, f32),
                pltpu.VMEM((length, deep, lanes), i32),
                pltpu.SMEM((length, deep, lanes), i32),
                pltpu.VMEM((depth, 2 * n_size), bf16),
                pltpu.VMEM((depth, 2 * n_size), bf16),
                pltpu.VMEM((4 * n_size, depth), bf16),
                pltpu.VMEM((2 * n_size, depth), bf16),
                pltpu.VMEM((depth, 2 * n_size), bf16),
                pltpu.VMEM((8, n_size), f32),
                pltpu.VMEM((count, 8, n_size), f32),
                dma((halves,)),
                dma((length, halves)),
                dma((length, halves)),
                dma((length, halves)),
                dma((length, halves)),
                dma((length,)),
                dma((length,)),
                dma((length,)),
                dma((length, columns, slots, halves)),
                dma((length, columns, slots, halves)),
                dma((count,)),
                dma((count,)),
            ],
            compiler_params=pltpu.CompilerParams(collective_id=0, has_side_effects=True, vmem_limit_bytes=60 << 20),
            name="step",
        )(up_index, down_index, occupation, bath_coef, bath_rate, step, lists, state, couplings, hamiltonian)

    return body


def solution(mesh):
    placed = (
        P(AXES, None, None, None),
        P(),
        P(),
        P(),
        P(),
        P(AXES, None),
        P(AXES, None, None),
        P(AXES, None),
        P(AXES, None),
        P(),
    )
    return jax.shard_map(
        make_body(mesh.shape["gx"], mesh.shape["gy"]),
        mesh=mesh,
        in_specs=placed,
        out_specs=(P(AXES, None, None, None), P(AXES, None, None, None)),
        check_vma=False,
    )
```

time: 143 us -> 114 us (0.80)
  waiting for transfers between devices: 69.5 us -> 0 us
  Pallas kernels: 52.6 us -> 108 us
  starting transfers between devices: 7.46 us -> 0 us
  local copies, waits for them, and re-layouts: 7.93 us -> 4.6 us
  other arithmetic: 3.24 us -> 0 us
    all_to_all x1 -> x0, waiting for transfers between devices: 69.5 us -> none  [body(): lax.all_to_all(outgoing, AXES, split_axis=0, concat_axis=0, tiled=True)]
    pallas_call x4 -> x1, Pallas kernels: 52.6 us -> 108 us  [body(): pl.pallas_call(functools.partial(kernel, gx, gy, length, halves), out_sha...]
    all_to_all x1 -> x0, starting transfers between devices: 7.46 us -> none  [body(): lax.all_to_all(outgoing, AXES, split_axis=0, concat_axis=0, tiled=True)]
    slice x3 -> x0, local copies, waits for them, and re-layouts: 3.39 us -> none  [the longest x1 1.2 us: body(): rms = jnp.sqrt(total[0, 0] / size + 1e-06)]
    add x1 -> x0, other arithmetic: 2.31 us -> none  [body(): advanced = state + step[0] / rms * derivative]
    unnamed x11 -> x6, local copies, waits for them, and re-layouts: 2.51 us -> 4.01 us
  transfers between devices with their start and end apart: 1 -> 0, of which waited for: 1 -> 0; matrix products, arithmetic and copies ran while one was open for 5% -> 0% of each run, Pallas kernels for 13% -> 0%
where the time goes in v2:
time: 114 us
  Pallas kernels  108 us (95%)
  local copies, waits for them, and re-layouts  4.6 us (4%)
  between operations  1.3 us (1%)
    pallas_call x1, Pallas kernels, body(): pl.pallas_call(functools.partial(kernel, gx, gy, length, halves), out_sha...  108 us
    unnamed x6, local copies, waits for them, and re-layouts  4.01 us

profile of v2, /device:TPU:0, one launch (start us, length us, event | category | flops | bytes accessed | tf_op | source)
XLA Modules:
  0.0 114.3 jit_solution(13545772724768125533)
XLA Ops:
  1.3 0.0 copy-start.1
  1.3 0.6 copy-done.1
  1.9 0.6 pad_bitcast_fusion.lists
  2.5 108.4 %step.2 = (f32[8,2,128,128]{3,2,1,0:T(8,128)}, f32[8,2,128,128]{3,2,1,0:T(8,128)}) custom-call(s32[8,16]{1,0:T(8,128)} %up.1, s32[8,16]{1,0:T(8,128)} %down.1, s32[8,16]{1,0:T(8,128)} %occ.1, f32[2,16]{1,0:T(2,128)} %coef.1, f32[16]{0:T(128)} %rate.1, f32[1]{0:T(128)S(6)} %copy.14.step, s32[8,128]{1,0:T(8,128)} %pad_bitcast_fusion.lists, ...), custom_call_target="tpu_custom_call" | custom-call | tf_op jit(solution)/shard_map/step/pallas_call | solution.py:372
  110.9 0.0 copy-start
  111.0 2.4 %copy.15 = f32[8,2,128,128]{3,2,1,0:T(8,128)} copy(f32[8,2,128,128]{3,2,1,0:T(8,128)} %get-tuple-element.4) | data formatting | bytes 2097152
  113.3 0.0 copy-done
  113.3 1.0 copy.16
Async XLA Ops:
  1.3 0.7 copy-start.1
  110.9 2.4 %copy-start = (f32[8,2,128,128]{3,2,1,0:T(8,128)S(1)}, f32[8,2,128,128]{3,2,1,0:T(8,128)}, u32[]{:S(2)}) copy-start(f32[8,2,128,128]{3,2,1,0:T(8,128)} %get-tuple-element.5) | copy-start | bytes 3145732

commit v3 on v2

--- a/solution.py
+++ b/solution.py
@@ -82,7 +82,7 @@
     gx, gy, length, halves,
     up, down, occ, coef, rate, step, lists, state, couplings, hamiltonian,
     derivative, advanced,
-    below, above, stage, arrived, list_v, list_s, x_hi, x_lo, y_all, q_left, q_right, squares, gathered,
+    below, above, stage, arrived, list_v, list_s, x_hi, x_lo, y_all, x_hi_2, x_lo_2, y_all_2, q_left, q_right, squares, gathered,
     load_sem, up_sem, down_sem, below_sem, above_sem, list_send, list_recv, list_load, plane_send, plane_recv, sum_send, sum_recv,
 ):
     rows, modes = up.shape
@@ -250,15 +250,16 @@
         copy.start()
         copy.wait()
 
-    share = rows // halves
-
-    for half in range(halves):
+    turns = 2 if rows % 2 == 0 and halves % 2 == 0 else 1
+    share, strips = rows // turns, halves // turns
+    for turn in range(turns):
 
         @pl.loop(0, share)
         def _(n):
-            local_part(half * share + n)
-
-        arrive(1, half)
+            local_part(turn * share + n)
+
+        for half in range(turn * strips, (turn + 1) * strips):
+            arrive(1, half)
 
     for hop in range(2, length):
         for half in range(halves):
@@ -275,16 +276,32 @@
     squares[...] = jnp.zeros_like(squares)
     depth = modes * n_size
 
-    @pl.loop(0, rows)
-    def _(n):
-        build_modes(n, rows, [arrived], up, down, occ, coef, x_hi, x_lo, y_all)
-        ops = (x_hi.at[:depth], x_lo.at[:depth], y_all.at[:, :depth], q_left.at[:, :depth], q_right.at[:depth])
-        re, im = products(n_size, *ops)
+    first = (x_hi.at[:depth], x_lo.at[:depth], y_all.at[:, :depth])
+    second = (x_hi_2, x_lo_2, y_all_2)
+
+    def build(n, operands):
+        build_modes(n, rows, [arrived], up, down, occ, coef, *operands)
+
+    def finish(n, operands):
+        re, im = products(n_size, *operands, q_left.at[:, :depth], q_right.at[:depth])
         re, im = derivative[n, 0] + im, derivative[n, 1] - re
         derivative[n, 0] = re
         derivative[n, 1] = im
         total = re * re + im * im
         squares[...] += jnp.sum(total.reshape(n_size // 8, 8, n_size), axis=0)
+
+    build(0, first)
+
+    @pl.loop(0, rows // 2)
+    def _(pair):
+        n = pair * 2
+        build(n + 1, second)
+        finish(n, first)
+        build(jnp.minimum(n + 2, rows - 1), first)
+        finish(n + 1, second)
+
+    if rows % 2:
+        finish(rows - 1, first)
 
     def copy_to(hop):
         other = lax.rem(me + hop, count)
@@ -358,7 +375,7 @@
         rows, parts, n_size, _ = state.shape
         modes = couplings.shape[0]
         slots = send_list.shape[2]
-        halves = 2 if rows % 2 == 0 and n_size % 16 == 0 else 1
+        halves = 4 if n_size % 32 == 0 else 1
         chosen = send_list.reshape(-1)
         lanes = 128
         deep = -(-chosen.shape[0] // (8 * lanes)) * 8
@@ -384,6 +401,9 @@
                 pltpu.VMEM((depth, 2 * n_size), bf16),
                 pltpu.VMEM((depth, 2 * n_size), bf16),
                 pltpu.VMEM((4 * n_size, depth), bf16),
+                pltpu.VMEM((modes * n_size, 2 * n_size), bf16),
+                pltpu.VMEM((modes * n_size, 2 * n_size), bf16),
+                pltpu.VMEM((4 * n_size, modes * n_size), bf16),
                 pltpu.VMEM((2 * n_size, depth), bf16),
                 pltpu.VMEM((depth, 2 * n_size), bf16),
                 pltpu.VMEM((8, n_size), f32),

time: 114 us -> 114 us (level)
  no operation moved by 1% of the time
where the time goes in v3:
time: 114 us
  Pallas kernels  108 us (95%)
  local copies, waits for them, and re-layouts  4.6 us (4%)
  between operations  1.3 us (1%)
    pallas_call x1, Pallas kernels, body(): pl.pallas_call(functools.partial(kernel, gx, gy, length, halves), out_sha...  108 us
    unnamed x6, local copies, waits for them, and re-layouts  4.01 us

profile of v3, /device:TPU:0, one launch (start us, length us, event | category | flops | bytes accessed | tf_op | source)
XLA Modules:
  0.0 113.9 jit_solution(4519168603550362069)
XLA Ops:
  1.3 0.0 copy-start.1
  1.3 0.6 copy-done.1
  1.9 0.6 pad_bitcast_fusion.lists
  2.5 108.0 %step.2 = (f32[8,2,128,128]{3,2,1,0:T(8,128)}, f32[8,2,128,128]{3,2,1,0:T(8,128)}) custom-call(s32[8,16]{1,0:T(8,128)} %up.1, s32[8,16]{1,0:T(8,128)} %down.1, s32[8,16]{1,0:T(8,128)} %occ.1, f32[2,16]{1,0:T(2,128)} %coef.1, f32[16]{0:T(128)} %rate.1, f32[1]{0:T(128)S(6)} %copy.14.step, s32[8,128]{1,0:T(8,128)} %pad_bitcast_fusion.lists, ...), custom_call_target="tpu_custom_call" | custom-call | tf_op jit(solution)/shard_map/step/pallas_call | solution.py:389
  110.5 0.0 copy-start
  110.5 2.4 %copy.15 = f32[8,2,128,128]{3,2,1,0:T(8,128)} copy(f32[8,2,128,128]{3,2,1,0:T(8,128)} %get-tuple-element.4) | data formatting | bytes 2097152
  112.9 0.0 copy-done
  112.9 1.0 copy.16
Async XLA Ops:
  1.3 0.7 copy-start.1
  110.5 2.4 %copy-start = (f32[8,2,128,128]{3,2,1,0:T(8,128)S(1)}, f32[8,2,128,128]{3,2,1,0:T(8,128)}, u32[]{:S(2)}) copy-start(f32[8,2,128,128]{3,2,1,0:T(8,128)} %get-tuple-element.5) | copy-start | bytes 3145732
